TPU v7x, 128 devices: a whole 4x4x4 slice. The times are simulated.
128 devices in a mesh: member: 8 (over y, z_lo), tile: 16 (over z_hi, x, core).
Axes of the slice: x: 4, y: 4, z: 4 (z_hi: 2, z_lo: 2; z = z_hi * 2 + z_lo), core: 2. Of those that a mesh axis runs over, the one named last changes fastest.
Arguments:
- northward_speed_field: float32 [32, 16, 128, 1024], P('member', None, 'tile'), may hold values from -6 to 6
- level_depth_extent: float32 [32, 16, 128, 1024], P('member', None, 'tile'), may hold values from 0.2 to 5
- potential_warmth_anomaly: float32 [32, 16, 128, 1024], P('member', None, 'tile'), may hold values from -6 to 6
- ocean_region_label: int32 [128, 1024], P('tile'), may hold values from 0 to 9
- zone_for_parallel: int32 [1024], replicated, may hold values from 0 to 15, never falling along the last dimension, each value on 1 to 128 neighbouring positions
Outputs:
- mean_psi: float32 [10, 16, 1024], P(None, None, ('member', 'tile'))
- mean_heat: float32 [10, 1024], P(None, ('member', 'tile'))
- covariance: float32 [16, 32, 32], replicated
Inputs may be any that keep to these rules, and one draw needn't show every extreme that they name: `zone_for_parallel`: never falls along latitude; every band holds 1 to 128 latitudes.
All inputs are finite; a program needn't handle non-finite values.
Results may differ from a plain program's by a relative error of at most 0.00011.
Values sent between devices are 32-bit elements; how exact they have to be, the bound alone decides.
A program may use at most 128 MiB of HBM per device.

v0:
```python
import math

import jax
import jax.numpy as jnp
from jax import lax
from jax.sharding import Mesh
from jax.sharding import PartitionSpec as P

BASINS = 10
NBANDS = 16
MEMBER = ("member_0", "member_1")
MEMBER_TILE = ("member_0", "member_1", "tile")


def in_blocks(x, dim, devices):
    before, after = (x.shape[:dim], x.shape[dim + 1 :])
    return jnp.moveaxis(x.reshape(*before, devices, -1, *after), dim, 0)


def sent_and_summed(x, axis, dim):
    devices = lax.axis_size(axis)
    parts = lax.all_to_all(in_blocks(x, dim, devices), axis, 0, 0, tiled=True)
    return jnp.sum(parts, axis=0)


def in_order(parts, dim):
    parts = jnp.moveaxis(parts, 0, dim)
    dims = parts.shape
    return parts.reshape(*dims[:dim], dims[dim] * dims[dim + 1], *dims[dim + 2 :])


def turned_blocks(parts, axes, turns):
    dims = [lax.axis_size(a) for a in axes]
    parts = parts.reshape(*dims, *parts.shape[1:])
    for k in turns:
        parts = lax.all_to_all(parts, axes[k], split_axis=k, concat_axis=k, tiled=True)
    return parts.reshape(-1, *parts.shape[len(axes) :])


def one_axis_at_a_time(x, axes, turns, split_dim, concat_dim):
    parts = in_blocks(x, split_dim, lax.axis_size(axes))
    return in_order(turned_blocks(parts, axes, turns), concat_dim)


def metric_factor(lats):
    index = jnp.arange(lats, dtype=jnp.float32)
    return jnp.cos((-80.0 + 160.0 * (index + 0.5) / lats) * (math.pi / 180.0))


def local(
    northward_speed_field,
    level_depth_extent,
    potential_warmth_anomaly,
    ocean_region_label,
    zone_for_parallel,
):
    greatest_bound_value = lax.Precision.HIGHEST
    members_here, layers, columns, lats = northward_speed_field.shape
    tiles = lax.axis_size("tile")
    groups = lax.axis_size(MEMBER)
    owned = lats // (groups * tiles)
    northward_volume_carriage = northward_speed_field * level_depth_extent * metric_factor(lats)
    region_indicator_matrix = (
        ocean_region_label[None, :, :] == jnp.arange(BASINS, dtype=jnp.int32)[:, None, None]
    ).astype(jnp.float32)
    transport = jnp.einsum(
        "mkxl,bxl->mbkl",
        northward_volume_carriage,
        region_indicator_matrix,
        precision=greatest_bound_value,
    ) / math.sqrt(columns * tiles)
    thermal_energy_integral = jnp.einsum(
        "tzux,pux->tpx",
        northward_volume_carriage * potential_warmth_anomaly,
        region_indicator_matrix,
        precision=greatest_bound_value,
    ) / math.sqrt(columns * tiles * layers)
    partial_value = jnp.concatenate(
        [transport.reshape(members_here, BASINS * layers, lats), thermal_energy_integral], axis=1
    )
    features = partial_value.shape[1]
    blocked = partial_value.reshape(members_here, features, groups, tiles, owned)
    blocked = jnp.transpose(blocked, (2, 3, 0, 1, 4)).reshape(
        groups, tiles, members_here * features * owned
    )
    reduced = sent_and_summed(blocked, "tile", 1)
    regrouped = one_axis_at_a_time(reduced, MEMBER, (0, 1), 0, 0)
    summed = regrouped.reshape(groups * members_here, features, owned)
    members = summed.shape[0]
    streams = jnp.cumsum(
        summed[:, : BASINS * layers].reshape(members, BASINS, layers, owned), axis=2
    )
    heat_all = summed[:, BASINS * layers :]
    mean_psi = jnp.mean(streams, axis=0)
    mean_heat = jnp.mean(heat_all, axis=0)
    anomaly = (streams - mean_psi).reshape(members, BASINS * layers, owned)
    start = (lax.axis_index(MEMBER) * tiles + lax.axis_index("tile")) * owned
    bands_here = lax.dynamic_slice_in_dim(zone_for_parallel, start, owned)
    band_hot = (bands_here[:, None] == jnp.arange(NBANDS, dtype=jnp.int32)[None, :]).astype(
        jnp.float32
    )
    products = jnp.einsum("mfl,nfl->lmn", anomaly, anomaly, precision=greatest_bound_value)
    norm = float((members - 1) * BASINS * layers * (lats // NBANDS))
    local_cov = jnp.einsum("lmn,lc->cmn", products, band_hot, precision=greatest_bound_value) / norm
    covariance = lax.psum(local_cov, MEMBER_TILE)
    return (mean_psi, mean_heat, covariance)


def solution(mesh):
    split = Mesh(mesh.devices.reshape(4, 2, mesh.shape["tile"]), ("member_0", "member_1", "tile"))
    return jax.shard_map(
        local,
        mesh=split,
        in_specs=(
            P(MEMBER, None, "tile", None),
            P(MEMBER, None, "tile", None),
            P(MEMBER, None, "tile", None),
            P("tile", None),
            P(),
        ),
        out_specs=(P(None, None, MEMBER_TILE), P(None, MEMBER_TILE), P()),
        check_vma=False,
    )
```

profile of v0, /device:TPU:1, one launch (start us, length us, event | category | flops | bytes accessed | tf_op | source)
XLA Modules:
  0.0 345.3 jit_solution(7260591670129801373)
XLA Ops:
  7.2 3.6 %multiply_reduce_fusion = (f32[4,8,1024]{2,1,0:T(8,128)S(1)}, f32[4,16,8,1024]{3,2,1,0:T(8,128)S(1)}) fusion(f32[4,16,8,1024]{3,2,1,0:T(8,128)} %param.7, f32[1024]{0:T(1024)S(1)} %multiply_cosine_fusion, f32[4,16,8,1024]{3,2,1,0:T(8,128)} %param.5, f32[4,16,8,1024]{3,2,1,0:T(8,128)} %param.6), kind=kLoop, calls=%fused_computation.7 | loop fusion | flops 2064384 | bytes 8523776 | tf_op jit(solution)/shard_map/tzux,pux->tpx/reduce_sum | solution.py:72
  10.8 13.7 %copy.23 = f32[4,16,8,1024]{1,2,0,3:T(8,128)} copy(f32[4,16,8,1024]{3,2,1,0:T(8,128)S(1)} %get-tuple-element.13) | data formatting | bytes 4194304 | tf_op jit(solution)/shard_map/mul | solution.py:62
  24.7 29.5 %multiply_bitcast_fusion = f32[4,10,16,1024]{2,1,0,3:T(8,128)} fusion(f32[4,16,8,1024]{1,2,0,3:T(8,128)} %copy.23, s32[8,1024]{0,1:T(8,128)S(1)} %copy.22), kind=kOutput, calls=%fused_computation | convolution fusion | flops 63651840 | bytes 4751360 | tf_op jit(solution)/shard_map/mkxl,bxl->mbkl/dot_general | solution.py:66
  54.2 22.2 %reshape.39 = f32[4,160,8,16,8]{1,0,4,3,2:T(4,128)} reshape(f32[4,10,16,1024]{2,1,0,3:T(8,128)} %multiply_bitcast_fusion) | data formatting | bytes 5242880 | tf_op jit(solution)/shard_map/concatenate | solution.py:78
  76.4 4.9 %copy.43 = f32[4,160,8,16,8]{1,4,3,2,0:T(8,128)} copy(f32[4,160,8,16,8]{1,0,4,3,2:T(4,128)} %reshape.39) | data formatting | bytes 5242880 | tf_op jit(solution)/shard_map/concatenate | solution.py:78
  81.3 0.8 copy.25
  82.1 6.0 %fusion.7 = f32[1024,10,4]{1,2,0:T(4,128)S(1)} fusion(f32[4,8,1024]{1,0,2:T(4,128)S(1)} %copy.25, s32[8,1024]{0,1:T(8,128)S(1)} %copy.22), kind=kOutput, calls=%fused_computation.11 | convolution fusion | flops 4055040 | bytes 327680 | tf_op jit(solution)/shard_map/tzux,pux->tpx/dot_general | solution.py:72
  88.5 1.9 copy-done
  90.4 2.8 maximum_bitcast_fusion
  93.2 15.7 %copy.27 = f32[8,16,4,170,8]{1,4,3,2,0:T(8,128)} copy(f32[8,16,4,170,8]{3,4,1,0,2:T(8,128)} %maximum_bitcast_fusion) | data formatting | bytes 5570560 | tf_op jit(solution)/shard_map/transpose | solution.py:83
  108.8 12.4 %copy.28 = f32[16,8,1,5440]{3,1,2,0:T(8,128)S(1)} copy(f32[16,8,1,5440]{0,3,1,2:T(8,128)} %bitcast.32) | data formatting | bytes 5570560 | tf_op jit(solution)/shard_map/transpose | solution.py:17
  121.2 45.2 %all_to_all.15 = f32[16,8,1,5440]{3,1,2,0:T(8,128)} all-to-all(f32[16,8,1,5440]{3,1,2,0:T(8,128)S(1)} %copy.28), channel_id=1, replica_groups=mesh['member_0'=4,'member_1'=2,'tile'=16] {'tile'}, dimensions={0} | all-to-all | bytes 5570560 | tf_op jit(solution)/shard_map/all_to_all | solution.py:22
  166.5 1.9 reduce_sum.37
  168.5 9.1 %all_to_all.16 = f32[4,2,1,1,5440]{4,1,3,2,0:T(2,128)S(1)} all-to-all(f32[4,2,1,1,5440]{4,1,3,2,0:T(2,128)S(1)} %reshape_reshape.7), channel_id=1, replica_groups=mesh['member_0'=4,'member_1'=2,'tile'=16] {'member_0'}, dimensions={0} | all-to-all | bytes 348160 | tf_op jit(solution)/shard_map/all_to_all | solution.py:36
  178.3 3.4 all-to-all-start.2
  181.8 0.8 dynamic_slice.3
  182.5 2.7 all-to-all-done.2
  185.4 1.5 reshape_reshape_reshape.3
  187.3 2.9 fusion.14
  190.2 3.0 copy.33
  193.5 1.2 fusion.8
  194.7 1.1 convolution_multiply_fusion
  197.2 139.4 %all-reduce.2.cloned.1.call-done = f32[16,32,32]{2,0,1:T(8,128)} async-done(((f32[16,32,32]{2,0,1:T(8,128)}), f32[16,32,32]{2,0,1:T(8,128)}) %all-reduce.2.cloned.1.call-update) | async-done | bytes 65552 | tf_op jit(solution)/shard_map/psum | solution.py:105
  336.7 1.7 copy.41
  (19 shorter events, 3.5 us)
Async XLA Ops:
  10.8 13.7 %copy-start.1 = (s32[8,1024]{1,0:T(8,128)S(1)}, s32[8,1024]{1,0:T(8,128)}, u32[]{:S(2)}) copy-start(s32[8,1024]{1,0:T(8,128)} %param.8) | copy-start | bytes 98308
  88.2 2.2 copy-start
  178.3 7.0 %all-to-all-start.2 = ((f32[4,2,1,1,5440]{4,0,3,2,1:T(4,128)}), f32[4,2,1,1,5440]{4,0,3,2,1:T(4,128)S(1)}, u32[]{:S(2)}, u32[]{:S(2)}) async-start(f32[4,2,1,1,5440]{4,0,3,2,1:T(4,128)} %copy.29), calls=%async_computation.2 | async-start | bytes 352256 | tf_op jit(solution)/shard_map/all_to_all | solution.py:36
  181.7 155.0 %all-reduce.2.cloned.1.call-start = ((), (), s32[]{:S(2)}) async-start(), calls=%async_computation.3 | async-start | bytes 524288 | tf_op jit(solution)/shard_map/psum | solution.py:105
Sparse Core Ops, SparseCore 0:
  196.0 140.6 all-reduce.1
where the time goes:
time: 346 us; the launch traced here: 345 us
  waiting for transfers between devices  142 us (41%)
  local copies, waits for them, and re-layouts  81.7 us (24%)
  blocking collectives  54.3 us (16%)
  matrix products  37.9 us (11%)
  between operations  14.2 us (4%)
  other arithmetic  11.6 us (3%)
  starting transfers between devices  3.47 us (1%)
    psum x1, waiting for transfers between devices, local(): covariance = lax.psum(local_cov, MEMBER_TILE)  139 us
    all_to_all x1, blocking collectives, sent_and_summed(): parts = lax.all_to_all(in_blocks(x, dim, devices), axis, 0, 0, tiled=True)  45.2 us
    dot_general x1, matrix products, local(): jnp.einsum('mkxl,bxl->mbkl', northward_volume_carriage, region_indicator_...  29.5 us
    concatenate x3, local copies, waits for them, and re-layouts, local(): jnp.concatenate([transport.reshape(members_here, BASINS * layers, lats),...  27.3 us
    transpose x1, local copies, waits for them, and re-layouts, local(): jnp.transpose(blocked, (2, 3, 0, 1, 4))  15.7 us
    mul x1, local copies, waits for them, and re-layouts, local(): northward_speed_field * level_depth_extent * metric_factor(lats)  13.7 us
    transpose x1, local copies, waits for them, and re-layouts, in_blocks(): return jnp.moveaxis(x.reshape(*before, devices, -1, *after), dim, 0)  12.4 us
    all_to_all x1, blocking collectives, turned_blocks(): lax.all_to_all(parts, axes[k], split_axis=k, concat_axis=k, tiled=True)  9.05 us
  transfers between devices with their start and end apart: 2, of which 2 were waited for; matrix products, arithmetic and copies ran while one was open for 1% of the time, Pallas kernels for 0%

commit v1 on v0

v1 whole, which is shorter than its diff:
```python
import math

import jax
import jax.numpy as jnp
from jax import lax
from jax.experimental import pallas as pl
from jax.experimental.pallas import tpu as pltpu
from jax.sharding import PartitionSpec as P

MESH = pl.DeviceIdType.MESH
F32 = jnp.float32
BF16 = jnp.bfloat16

LANES = 128
BASINS = 10
LAYERS = 16
NBANDS = 16
MEMBERS = 32
GROUPS = 8
MINE = MEMBERS // GROUPS
COLS = 8
ROWS = BASINS + 1
PAD = 16
RING = 4
PEERS = 8
SPREAD = 16


def metric_factor(lats):
    index = jnp.arange(lats, dtype=F32)
    return jnp.cos((-80.0 + 160.0 * (index + 0.5) / lats) * (math.pi / 180.0))


def kernel(
    v_hbm, h_hbm, t_hbm, lab_ref, zone_ref, sp_ref,
    psi_out, heat_out, cov_out,
    vb, hb, tb, onehot, heat_cols, ps, cr, xs, fa, fb, na, nb, rl, ys, rb,
    an, pp, dd, c1, s1, c2, s2, df, mb, mm,
    hbm_sem, core_s, core_r, x_s, x_r, yz_s, yz_r,
    c1_s, c1_r, c2_s, c2_r, c3_s, c3_r, m1_s, m1_r, m2_s, m2_r,
):
    member = lax.axis_index("member")
    tile = lax.axis_index("tile")
    z_hi = tile // PEERS
    e = tile % PEERS
    x = e // 2
    core = e % 2
    me = z_hi * GROUPS + member

    def peer(i):
        other = lax.rem(e + i, PEERS)
        return other, {"member": member, "tile": z_hi * PEERS + other}

    def spread(i):
        other = lax.rem(me + i, SPREAD)
        return other, {"member": other % GROUPS, "tile": (other // GROUPS) * PEERS + e}

    def along_x(step):
        other = lax.rem(x + RING + step, RING)
        return {"member": member, "tile": z_hi * PEERS + other * 2 + core}

    sibling = {"member": member, "tile": z_hi * PEERS + x * 2 + (1 - core)}

    def remote(src, dst, send, recv, device):
        return pltpu.make_async_remote_copy(
            src_ref=src, dst_ref=dst, send_sem=send, recv_sem=recv,
            device_id=device, device_id_type=MESH,
        )

    chunk = LAYERS * COLS * 8

    def load(m):
        rows = pl.ds(m * chunk, chunk)
        return [
            pltpu.make_async_copy(a.at[rows], b.at[rows], hbm_sem.at[m, i])
            for i, (a, b) in enumerate(((v_hbm, vb), (h_hbm, hb), (t_hbm, tb)))
        ]

    for m in range(2):
        for c in load(m):
            c.start()

    barrier = pltpu.get_barrier_semaphore()

    @pl.loop(1, PEERS)
    def _(i):
        pl.semaphore_signal(barrier, inc=1, device_id=peer(i)[1], device_id_type=MESH)

    @pl.loop(1, SPREAD)
    def _(i):
        pl.semaphore_signal(barrier, inc=1, device_id=spread(i)[1], device_id_type=MESH)

    for col in range(COLS):
        lab = lab_ref[pl.ds(col, 8, stride=8), :]
        for b in range(BASINS):
            onehot[col * BASINS + b] = jnp.where(lab == b, 1.0, 0.0).astype(F32)
    zero = jnp.zeros((8, LANES), F32)
    for col in range(COLS):
        heat_cols[col] = zero

    def rows_of(m):
        return ROWS if m == MINE - 1 else BASINS

    def compute(m):
        for c in load(m):
            c.wait()
        if m + 2 < MINE:
            for c in load(m + 2):
                c.start()

        def body(kk, carry):
            acc, hs = list(carry[0]), list(carry[1])
            nxt = [None] * BASINS
            for col in range(COLS):
                base = m * chunk + kk * (2 * COLS * 8) + col
                first = pl.ds(base, 8, stride=8)
                second = pl.ds(base + COLS * 8, 8, stride=8)
                u0 = vb[first, :] * hb[first, :]
                u1 = vb[second, :] * hb[second, :]
                hs[col] = hs[col] + (u0 * tb[first, :] + u1 * tb[second, :])
                for b in range(BASINS):
                    o = onehot[col * BASINS + b]
                    acc[b] = acc[b] + o * u0
                    nxt[b] = o * u1 if nxt[b] is None else nxt[b] + o * u1
            for b in range(BASINS):
                ps[m, 0, kk, b] = acc[b]
                acc[b] = acc[b] + nxt[b]
                ps[m, 1, kk, b] = acc[b]
            return tuple(acc), tuple(hs)

        start = (tuple(zero for _ in range(BASINS)), tuple(heat_cols[c] for c in range(COLS)))
        _, hs = lax.fori_loop(0, LAYERS // 2, body, start)
        if m < MINE - 1:
            for col in range(COLS):
                heat_cols[col] = hs[col]
        else:
            for k in range(LAYERS):
                row = zero
                if k < BASINS:
                    for col in range(COLS):
                        row = row + onehot[col * BASINS + k] * hs[col]
                ps[m, k % 2, k // 2, BASINS] = row

    def core_copy(m):
        n = rows_of(m)
        return remote(
            ps.at[m, 1 - core, :, pl.ds(0, n)], cr.at[m, :, pl.ds(0, n)],
            core_s.at[m], core_r.at[m], sibling,
        )

    right, left = along_x(1), along_x(-1)
    at_right = lax.rem(x + 1, RING)
    at_left = lax.rem(x + 3, RING)
    at_far = lax.rem(x + 2, RING)

    def x_copies(m):
        n = pl.ds(0, rows_of(m))
        hi = RING

        def c(i, src, dst, device):
            return lambda: remote(src, dst, x_s.at[m, i], x_r.at[m, i], device)

        return dict(
            far_right=c(0, xs.at[m, at_far, n], fa.at[m, n], right),
            far_left=c(1, xs.at[m, hi + at_far, n], fb.at[m, n], left),
            near_right=c(2, xs.at[m, hi + at_right, n], na.at[m, 1, n], right),
            near_left=c(3, xs.at[m, at_left, n], nb.at[m, 0, n], left),
            sum_right=c(4, rl.at[m, 0, n], na.at[m, 0, n], right),
            sum_left=c(5, rl.at[m, 1, n], nb.at[m, 1, n], left),
        )

    def pair_sum(m):
        core_copy(m).wait_recv()
        n = rows_of(m)

        def one(kk, _):
            for r in range(n):
                xs[m, kk, r] = ps[m, core, kk, r] + cr[m, kk, r]
            return 0

        copies = x_copies(m)
        lax.fori_loop(0, LAYERS // 2, one, 0)
        for name in ("far_right", "far_left", "near_right", "near_left"):
            copies[name]().start()

    def relay(m):
        copies = x_copies(m)
        n = rows_of(m)
        copies["far_right"]().wait_recv()
        for r in range(n):
            rl[m, 0, r] = xs[m, at_right, r] + fa[m, r]
        copies["sum_right"]().start()
        copies["far_left"]().wait_recv()
        for r in range(n):
            rl[m, 1, r] = xs[m, RING + at_left, r] + fb[m, r]
        copies["sum_left"]().start()

    def piece(ref, i):
        return ref.at[pl.ds(pl.multiple_of(i * PAD, PAD), PAD)]

    def spread_out(m):
        copies = x_copies(m)
        n = rows_of(m)
        for name in ("near_right", "near_left", "sum_right", "sum_left"):
            copies[name]().wait_recv()
        for z in range(2):
            for r in range(n):
                total = xs[m, z * RING + x, r] + (na[m, z, r] + nb[m, z, r])
                ys[pl.ds((m * SPREAD + z * GROUPS) * PAD + r, 8, stride=PAD), :] = total
        for r in range(n, PAD):
            for z in range(2):
                ys[pl.ds((m * SPREAD + z * GROUPS) * PAD + r, 8, stride=PAD), :] = zero

        @pl.loop(1, SPREAD)
        def _(i):
            other, device = spread(i)
            remote(
                piece(ys, m * SPREAD + other), piece(rb, me * MINE + m),
                yz_s.at[m], yz_r.at[m], device,
            ).start()

        piece(rb, me * MINE + m)[...] = piece(ys, m * SPREAD + me)[...]

    def wait_bytes(ref, rows, sem):
        view = ref.at[pl.ds(0, rows)]
        pltpu.make_async_copy(view, view, sem).wait()

    compute(0)
    pl.semaphore_wait(barrier, PEERS - 1 + SPREAD - 1)
    core_copy(0).start()
    compute(1)
    core_copy(1).start()
    pair_sum(0)
    compute(2)
    core_copy(2).start()
    pair_sum(1)
    relay(0)
    compute(3)
    core_copy(3).start()
    pair_sum(2)
    relay(1)
    pair_sum(3)
    spread_out(0)
    relay(2)
    spread_out(1)
    relay(3)
    spread_out(2)
    spread_out(3)
    for m in range(MINE):
        wait_bytes(ys, (SPREAD - 1) * PAD, yz_r.at[m])

    spacing = jnp.broadcast_to(sp_ref[pl.ds(member, 1), :], (8, LANES))
    for b in range(BASINS):
        a = []
        for q in range(4):
            lo = rb[pl.ds(q * 8 * PAD + b, 8, stride=PAD), :]
            hi = rb[pl.ds((MEMBERS + q * 8) * PAD + b, 8, stride=PAD), :]
            a.append((lo + hi) * spacing)
        mean = jnp.sum((a[0] + a[1]) + (a[2] + a[3]), axis=0, keepdims=True) * (1.0 / MEMBERS)
        mb[pl.ds(b, 1), :] = mean
        for q in range(4):
            an[pl.ds(b * MEMBERS + q * 8, 8), :] = a[q] - mean
    last = (MINE - 1) * PAD + BASINS
    warm = rb[pl.ds(last, 8, stride=MINE * PAD), :] + rb[
        pl.ds(last + GROUPS * MINE * PAD, 8, stride=MINE * PAD), :
    ]
    warm = jnp.sum(warm * spacing, axis=0, keepdims=True)
    mb[pl.ds(BASINS, 1), :] = warm * (1.0 / (MEMBERS * math.sqrt(LAYERS)))
    for r in range(ROWS, PAD):
        mb[pl.ds(r, 1), :] = jnp.zeros((1, LANES), F32)

    mm[pl.ds(pl.multiple_of((e * 2 + z_hi) * PAD, PAD), PAD), :] = mb[...]
    means_over = remote(
        mb, piece(mm, e * 2 + z_hi), m1_s, m1_r,
        {"member": member, "tile": (1 - z_hi) * PEERS + e},
    )
    means_over.start()

    def gram(n, _):
        acc = [None] * 4
        for b in range(BASINS):
            row = jnp.broadcast_to(an[pl.ds(b * MEMBERS + n, 1), :], (8, LANES))
            for q in range(4):
                t = row * an[pl.ds(b * MEMBERS + q * 8, 8), :]
                acc[q] = t if acc[q] is None else acc[q] + t
        at = pl.multiple_of((n % 8) * LANES + (n // 8) * MEMBERS, MEMBERS)
        for q in range(4):
            pp[pl.ds(at + q * 8, 8), :] = acc[q]
        return 0

    lax.fori_loop(0, MEMBERS, gram, 0)

    zone = jnp.broadcast_to(zone_ref[pl.ds(member, 1), :], (NBANDS, LANES))
    band = jnp.where(
        zone == lax.broadcasted_iota(jnp.int32, (NBANDS, LANES), 0), 1.0, 0.0
    ).astype(BF16)
    for r in range(8):
        p = pp[pl.ds(r * LANES, LANES), :]
        total = None
        for _ in range(3):
            part = p.astype(BF16)
            p = p - part.astype(F32)
            d = lax.dot_general(
                band, part, (((1,), (1,)), ((), ())), preferred_element_type=F32
            )
            total = d if total is None else total + d
        dd[pl.ds(r * PAD, PAD), :] = total

    @pl.loop(1, PEERS)
    def _(i):
        other, device = peer(i)
        remote(piece(dd, other), piece(c1, e), c1_s, c1_r, device).start()

    means_over.wait_recv()
    both = pl.ds(pl.multiple_of(e * 2 * PAD, PAD), 2 * PAD)

    @pl.loop(1, PEERS)
    def _(i):
        remote(mm.at[both], mm.at[both], m2_s, m2_r, peer(i)[1]).start()

    piece(c1, e)[...] = piece(dd, e)[...]
    wait_bytes(c1, (PEERS - 1) * PAD, c1_r)
    total = c1[pl.ds(0, PAD), :]
    for i in range(1, PEERS):
        total = total + c1[pl.ds(i * PAD, PAD), :]
    s1[...] = total

    @pl.loop(1, SPREAD)
    def _(i):
        remote(s1, piece(c2, me), c2_s, c2_r, spread(i)[1]).start()

    piece(c2, me)[...] = total

    wait_bytes(mm, (PEERS - 1) * 2 * PAD, m2_r)
    turn = lax.rem(LANES - tile * 8, LANES)

    def mine(rows):
        return pltpu.roll(rows, turn, 1)[:, :8]

    for b in range(BASINS):
        for z in range(2):
            rows = mm[pl.ds(z * PAD + b, 8, stride=2 * PAD), :]
            psi_out[b, pl.ds(z * 8, 8), :] = mine(rows)
    heat_out[pl.ds(0, 8), :] = mine(mm[pl.ds(BASINS, 8, stride=2 * PAD), :])
    heat_out[pl.ds(8, 2), :] = mine(mm[pl.ds(PAD + BASINS, 8, stride=2 * PAD), :])[:2]

    wait_bytes(c2, (SPREAD - 1) * PAD, c2_r)
    total = c2[pl.ds(0, PAD), :]
    for i in range(1, SPREAD):
        total = total + c2[pl.ds(i * PAD, PAD), :]
    norm = float((MEMBERS - 1) * BASINS * LAYERS * (8 * LANES // NBANDS))
    s2[...] = total * (1.0 / norm)

    @pl.loop(1, PEERS)
    def _(i):
        remote(s2, piece(df, e), c3_s, c3_r, peer(i)[1]).start()

    piece(df, e)[...] = s2[...]

    for m in range(MINE):
        core_copy(m).wait_send()
        for c in x_copies(m).values():
            c().wait_send()
        wait_bytes(ys, (SPREAD - 1) * PAD, yz_s.at[m])
    means_over.wait_send()
    wait_bytes(c1, (PEERS - 1) * PAD, c1_s)
    wait_bytes(mm, (PEERS - 1) * 2 * PAD, m2_s)
    wait_bytes(c2, (SPREAD - 1) * PAD, c2_s)
    wait_bytes(df, (PEERS - 1) * PAD, c3_s)

    wait_bytes(df, (PEERS - 1) * PAD, c3_r)
    for c in range(NBANDS):
        rows = df[pl.ds(c, 8, stride=PAD), :]
        for q in range(4):
            part = rows if q == 0 else pltpu.roll(rows, LANES - MEMBERS * q, 1)
            cov_out[c, pl.ds(q * 8, 8), :] = part[:, :MEMBERS]


def lat_tiles(a):
    *lead, cols, lats = a.shape
    a = a.reshape(*lead, cols, lats // LANES, LANES)
    a = jnp.swapaxes(a, -3, -2)
    return a.reshape(-1, LANES)


def local(v, h, t, lab, zone):
    lats = v.shape[-1]
    columns = COLS * 16
    spacing = (metric_factor(lats) / math.sqrt(columns)).reshape(8, LANES)
    vmem = lambda *s: pltpu.VMEM(s, F32)
    big = MINE * LAYERS * COLS * 8
    dma = pltpu.SemaphoreType.DMA
    anywhere = pl.BlockSpec(memory_space=pl.ANY)
    inside = pl.BlockSpec(memory_space=pltpu.VMEM)
    psi, heat, cov = pl.pallas_call(
        kernel,
        out_shape=(
            jax.ShapeDtypeStruct((BASINS, LAYERS, 8), F32),
            jax.ShapeDtypeStruct((BASINS, 8), F32),
            jax.ShapeDtypeStruct((NBANDS, MEMBERS, MEMBERS), F32),
        ),
        in_specs=[anywhere] * 3 + [inside] * 3,
        out_specs=(inside, inside, inside),
        scratch_shapes=[
            vmem(big, LANES), vmem(big, LANES), vmem(big, LANES),
            vmem(COLS * BASINS, 8, LANES),
            vmem(COLS, 8, LANES),
            vmem(MINE, 2, LAYERS // 2, ROWS, 8, LANES),
            vmem(MINE, LAYERS // 2, ROWS, 8, LANES),
            vmem(MINE, LAYERS // 2, ROWS, 8, LANES),
            vmem(MINE, ROWS, 8, LANES),
            vmem(MINE, ROWS, 8, LANES),
            vmem(MINE, 2, ROWS, 8, LANES),
            vmem(MINE, 2, ROWS, 8, LANES),
            vmem(MINE, 2, ROWS, 8, LANES),
            vmem(MINE * SPREAD * PAD, LANES),
            vmem(MINE * SPREAD * PAD, LANES),
            vmem(BASINS * MEMBERS, LANES),
            vmem(MEMBERS * MEMBERS, LANES),
            vmem(PEERS * PAD, LANES),
            vmem(PEERS * PAD, LANES),
            vmem(PAD, LANES),
            vmem(SPREAD * PAD, LANES),
            vmem(PAD, LANES),
            vmem(PEERS * PAD, LANES),
            vmem(PAD, LANES),
            vmem(PEERS * 2 * PAD, LANES),
            dma((MINE, 3)),
            dma((MINE,)), dma((MINE,)),
            dma((MINE, 6)), dma((MINE, 6)),
            dma((MINE,)), dma((MINE,)),
            dma, dma, dma, dma, dma, dma, dma, dma, dma, dma,
        ],
        compiler_params=pltpu.CompilerParams(collective_id=0, has_side_effects=True),
        name="overturning",
    )(lat_tiles(v), lat_tiles(h), lat_tiles(t), lat_tiles(lab), zone.reshape(8, LANES), spacing)
    return psi, heat, cov


def solution(mesh):
    return jax.shard_map(
        local,
        mesh=mesh,
        in_specs=(
            P("member", None, "tile", None),
            P("member", None, "tile", None),
            P("member", None, "tile", None),
            P("tile", None),
            P(),
        ),
        out_specs=(
            P(None, None, ("member", "tile")),
            P(None, ("member", "tile")),
            P(),
        ),
        check_vma=False,
    )
```

time: 346 us -> 51.7 us (0.15)
  waiting for transfers between devices: 142 us -> 0 us
  local copies, waits for them, and re-layouts: 81.7 us -> 4.62 us
  blocking collectives: 54.3 us -> 0 us
  Pallas kernels: 0 us -> 45.5 us
  matrix products: 37.9 us -> 0 us
  between operations: 14.2 us -> 0.64 us
  other arithmetic: 11.6 us -> 0.65 us
  starting transfers between devices: 3.47 us -> 0 us
    psum x1 -> x0, waiting for transfers between devices: 139 us -> none  [local(): covariance = lax.psum(local_cov, MEMBER_TILE)]
    all_to_all x2 -> x0, blocking collectives: 54.3 us -> none  [the longest x1 45.2 us: sent_and_summed(): parts = lax.all_to_all(in_blocks(x, dim, devices), axis, 0, 0, tiled=True)]
    pallas_call x0 -> x1, Pallas kernels: none -> 45.5 us  [local(): pl.pallas_call(kernel, out_shape=(jax.ShapeDtypeStruct((BASINS, LAYERS, 8...]
    dot_general x4 -> x0, matrix products: 37.9 us -> none  [the longest x1 29.5 us: local(): jnp.einsum('mkxl,bxl->mbkl', northward_volume_carriage, region_indicator_...]
    transpose x2 -> x0, local copies, waits for them, and re-layouts: 28 us -> none  [the longest x1 15.7 us: local(): jnp.transpose(blocked, (2, 3, 0, 1, 4))]
    concatenate x3 -> x0, local copies, waits for them, and re-layouts: 27.3 us -> none  [local(): jnp.concatenate([transport.reshape(members_here, BASINS * layers, lats),...]
    mul x1 -> x0, local copies, waits for them, and re-layouts: 13.7 us -> none  [local(): northward_speed_field * level_depth_extent * metric_factor(lats)]
    reduce_sum x3 -> x0, other arithmetic: 5.6 us -> none  [the longest x1 3.61 us: local(): jnp.einsum('tzux,pux->tpx', northward_volume_carriage * potential_warmth_...]
  transfers between devices with their start and end apart: 2 -> 0, of which waited for: 2 -> 0; matrix products, arithmetic and copies ran while one was open for 1% -> 0% of each run, Pallas kernels for 0% -> 0%
where the time goes in v1:
time: 51.7 us; the launch traced here: 51.4 us
  Pallas kernels  45.5 us (88%)
  local copies, waits for them, and re-layouts  4.62 us (9%)
  other arithmetic  0.65 us (1%)
  between operations  0.64 us (1%)
    pallas_call x1, Pallas kernels, local(): pl.pallas_call(kernel, out_shape=(jax.ShapeDtypeStruct((BASINS, LAYERS, 8...  45.5 us
    pallas_call x2, local copies, waits for them, and re-layouts, local(): pl.pallas_call(kernel, out_shape=(jax.ShapeDtypeStruct((BASINS, LAYERS, 8...  2.95 us
    unnamed x1, local copies, waits for them, and re-layouts  1.67 us

profile of v1, /device:TPU:1, one launch (start us, length us, event | category | flops | bytes accessed | tf_op | source)
XLA Modules:
  0.0 51.4 jit_solution(4615100594971645546)
XLA Ops:
  0.6 0.6 %cosine_multiply_fusion.sp_ref = f32[8,128]{1,0:T(8,128)} fusion(), kind=kLoop, calls=%fused_computation | loop fusion | flops 7168 | bytes 4096 | tf_op jit(solution)/shard_map/div | solution.py:389
  1.3 45.5 %overturning.1 = (f32[10,16,8]{2,1,0:T(8,128)}, f32[10,8]{1,0:T(8,128)}, f32[16,32,32]{2,1,0:T(8,128)}) custom-call(f32[4096,128]{1,0:T(8,128)} %bitcast.21, f32[4096,128]{1,0:T(8,128)} %bitcast.22, f32[4096,128]{1,0:T(8,128)} %bitcast.23, s32[64,128]{1,0:T(8,128)} %bitcast.24, s32[8,128]{1,0:T(8,128)} %bitcast.25, f32[8,128]{1,0:T(8,128)} %cosine_multiply_fusion.sp_ref), custom_call_target="tpu_custom_call" | custom-call | tf_op jit(solution)/shard_map/overturning/pallas_call | solution.py:395
  46.8 1.6 %copy.8 = f32[10,16,8]{1,2,0:T(8,128)} copy(f32[10,16,8]{2,1,0:T(8,128)} %get-tuple-element.3) | data formatting | bytes 10240 | tf_op jit(solution)/shard_map/overturning/pallas_call | solution.py:395
  48.4 1.4 %copy.9 = f32[10,8]{0,1:T(8,128)} copy(f32[10,8]{1,0:T(8,128)} %get-tuple-element.4) | data formatting | bytes 640 | tf_op jit(solution)/shard_map/overturning/pallas_call | solution.py:395
  49.7 1.7 %copy.11 = f32[16,32,32]{2,1,0:T(8,128)} copy(f32[16,32,32]{2,1,0:T(8,128)} %get-tuple-element.11) | data formatting | bytes 131072

commit v2 on v1

--- a/solution.py
+++ b/solution.py
@@ -26,17 +26,19 @@
 SPREAD = 16
 
 
-def metric_factor(lats):
-    index = jnp.arange(lats, dtype=F32)
-    return jnp.cos((-80.0 + 160.0 * (index + 0.5) / lats) * (math.pi / 180.0))
+def metric_factor(row):
+    lats = 8 * LANES
+    index = lax.broadcasted_iota(jnp.int32, (8, LANES), 1) + row * LANES
+    degrees = -80.0 + 160.0 * (index.astype(F32) + 0.5) / lats
+    return jnp.cos(degrees * (math.pi / 180.0)) * (1.0 / math.sqrt(COLS * 16))
 
 
 def kernel(
-    v_hbm, h_hbm, t_hbm, lab_ref, zone_ref, sp_ref,
+    v_hbm, h_hbm, t_hbm, lab_hbm, zone_hbm,
     psi_out, heat_out, cov_out,
-    vb, hb, tb, onehot, heat_cols, ps, cr, xs, fa, fb, na, nb, rl, ys, rb,
+    vb, hb, tb, lab_ref, zone_ref, onehot, heat_cols, ps, cr, xs, fa, fb, na, nb, rl, ys, rb,
     an, pp, dd, c1, s1, c2, s2, df, mb, mm,
-    hbm_sem, core_s, core_r, x_s, x_r, yz_s, yz_r,
+    hbm_sem, small_sem, core_s, core_r, x_s, x_r, yz_s, yz_r,
     c1_s, c1_r, c2_s, c2_r, c3_s, c3_r, m1_s, m1_r, m2_s, m2_r,
 ):
     member = lax.axis_index("member")
@@ -76,9 +78,13 @@
             for i, (a, b) in enumerate(((v_hbm, vb), (h_hbm, hb), (t_hbm, tb)))
         ]
 
+    labels = pltpu.make_async_copy(lab_hbm, lab_ref, small_sem.at[0])
+    zones = pltpu.make_async_copy(zone_hbm, zone_ref, small_sem.at[1])
+    labels.start()
     for m in range(2):
         for c in load(m):
             c.start()
+    zones.start()
 
     barrier = pltpu.get_barrier_semaphore()
 
@@ -90,6 +96,7 @@
     def _(i):
         pl.semaphore_signal(barrier, inc=1, device_id=spread(i)[1], device_id_type=MESH)
 
+    labels.wait()
     for col in range(COLS):
         lab = lab_ref[pl.ds(col, 8, stride=8), :]
         for b in range(BASINS):
@@ -102,8 +109,9 @@
         return ROWS if m == MINE - 1 else BASINS
 
     def compute(m):
-        for c in load(m):
-            c.wait()
+        with jax.named_scope("hbm_wait"):
+            for c in load(m):
+                c.wait()
         if m + 2 < MINE:
             for c in load(m + 2):
                 c.start()
@@ -129,7 +137,8 @@
             return tuple(acc), tuple(hs)
 
         start = (tuple(zero for _ in range(BASINS)), tuple(heat_cols[c] for c in range(COLS)))
-        _, hs = lax.fori_loop(0, LAYERS // 2, body, start)
+        with jax.named_scope("zonal"):
+            _, hs = lax.fori_loop(0, LAYERS // 2, body, start)
         if m < MINE - 1:
             for col in range(COLS):
                 heat_cols[col] = hs[col]
@@ -170,7 +179,8 @@
         )
 
     def pair_sum(m):
-        core_copy(m).wait_recv()
+        with jax.named_scope("core_wait"):
+            core_copy(m).wait_recv()
         n = rows_of(m)
 
         def one(kk, _):
@@ -179,18 +189,21 @@
             return 0
 
         copies = x_copies(m)
-        lax.fori_loop(0, LAYERS // 2, one, 0)
+        with jax.named_scope("pair_sum"):
+            lax.fori_loop(0, LAYERS // 2, one, 0)
         for name in ("far_right", "far_left", "near_right", "near_left"):
             copies[name]().start()
 
     def relay(m):
         copies = x_copies(m)
         n = rows_of(m)
-        copies["far_right"]().wait_recv()
+        with jax.named_scope("far_wait"):
+            copies["far_right"]().wait_recv()
         for r in range(n):
             rl[m, 0, r] = xs[m, at_right, r] + fa[m, r]
         copies["sum_right"]().start()
-        copies["far_left"]().wait_recv()
+        with jax.named_scope("far_wait"):
+            copies["far_left"]().wait_recv()
         for r in range(n):
             rl[m, 1, r] = xs[m, RING + at_left, r] + fb[m, r]
         copies["sum_left"]().start()
@@ -201,8 +214,9 @@
     def spread_out(m):
         copies = x_copies(m)
         n = rows_of(m)
-        for name in ("near_right", "near_left", "sum_right", "sum_left"):
-            copies[name]().wait_recv()
+        with jax.named_scope("near_wait"):
+            for name in ("near_right", "near_left", "sum_right", "sum_left"):
+                copies[name]().wait_recv()
         for z in range(2):
             for r in range(n):
                 total = xs[m, z * RING + x, r] + (na[m, z, r] + nb[m, z, r])
@@ -225,8 +239,11 @@
         view = ref.at[pl.ds(0, rows)]
         pltpu.make_async_copy(view, view, sem).wait()
 
+    spacing = metric_factor(member)
+
     compute(0)
-    pl.semaphore_wait(barrier, PEERS - 1 + SPREAD - 1)
+    with jax.named_scope("entry"):
+        pl.semaphore_wait(barrier, PEERS - 1 + SPREAD - 1)
     core_copy(0).start()
     compute(1)
     core_copy(1).start()
@@ -246,28 +263,29 @@
     relay(3)
     spread_out(2)
     spread_out(3)
-    for m in range(MINE):
-        wait_bytes(ys, (SPREAD - 1) * PAD, yz_r.at[m])
-
-    spacing = jnp.broadcast_to(sp_ref[pl.ds(member, 1), :], (8, LANES))
-    for b in range(BASINS):
-        a = []
-        for q in range(4):
-            lo = rb[pl.ds(q * 8 * PAD + b, 8, stride=PAD), :]
-            hi = rb[pl.ds((MEMBERS + q * 8) * PAD + b, 8, stride=PAD), :]
-            a.append((lo + hi) * spacing)
-        mean = jnp.sum((a[0] + a[1]) + (a[2] + a[3]), axis=0, keepdims=True) * (1.0 / MEMBERS)
-        mb[pl.ds(b, 1), :] = mean
-        for q in range(4):
-            an[pl.ds(b * MEMBERS + q * 8, 8), :] = a[q] - mean
-    last = (MINE - 1) * PAD + BASINS
-    warm = rb[pl.ds(last, 8, stride=MINE * PAD), :] + rb[
-        pl.ds(last + GROUPS * MINE * PAD, 8, stride=MINE * PAD), :
-    ]
-    warm = jnp.sum(warm * spacing, axis=0, keepdims=True)
-    mb[pl.ds(BASINS, 1), :] = warm * (1.0 / (MEMBERS * math.sqrt(LAYERS)))
-    for r in range(ROWS, PAD):
-        mb[pl.ds(r, 1), :] = jnp.zeros((1, LANES), F32)
+    with jax.named_scope("yz_wait"):
+        for m in range(MINE):
+            wait_bytes(ys, (SPREAD - 1) * PAD, yz_r.at[m])
+
+    with jax.named_scope("anomaly"):
+        for b in range(BASINS):
+            a = []
+            for q in range(4):
+                lo = rb[pl.ds(q * 8 * PAD + b, 8, stride=PAD), :]
+                hi = rb[pl.ds((MEMBERS + q * 8) * PAD + b, 8, stride=PAD), :]
+                a.append((lo + hi) * spacing)
+            mean = jnp.sum((a[0] + a[1]) + (a[2] + a[3]), axis=0, keepdims=True) * (1.0 / MEMBERS)
+            mb[pl.ds(b, 1), :] = mean
+            for q in range(4):
+                an[pl.ds(b * MEMBERS + q * 8, 8), :] = a[q] - mean
+        last = (MINE - 1) * PAD + BASINS
+        warm = rb[pl.ds(last, 8, stride=MINE * PAD), :] + rb[
+            pl.ds(last + GROUPS * MINE * PAD, 8, stride=MINE * PAD), :
+        ]
+        warm = jnp.sum(warm * spacing, axis=0, keepdims=True)
+        mb[pl.ds(BASINS, 1), :] = warm * (1.0 / (MEMBERS * math.sqrt(LAYERS)))
+        for r in range(ROWS, PAD):
+            mb[pl.ds(r, 1), :] = jnp.zeros((1, LANES), F32)
 
     mm[pl.ds(pl.multiple_of((e * 2 + z_hi) * PAD, PAD), PAD), :] = mb[...]
     means_over = remote(
@@ -288,38 +306,35 @@
             pp[pl.ds(at + q * 8, 8), :] = acc[q]
         return 0
 
-    lax.fori_loop(0, MEMBERS, gram, 0)
-
+    with jax.named_scope("gram"):
+        lax.fori_loop(0, MEMBERS, gram, 0)
+
+    zones.wait()
     zone = jnp.broadcast_to(zone_ref[pl.ds(member, 1), :], (NBANDS, LANES))
     band = jnp.where(
         zone == lax.broadcasted_iota(jnp.int32, (NBANDS, LANES), 0), 1.0, 0.0
     ).astype(BF16)
-    for r in range(8):
-        p = pp[pl.ds(r * LANES, LANES), :]
-        total = None
-        for _ in range(3):
-            part = p.astype(BF16)
-            p = p - part.astype(F32)
-            d = lax.dot_general(
-                band, part, (((1,), (1,)), ((), ())), preferred_element_type=F32
-            )
-            total = d if total is None else total + d
-        dd[pl.ds(r * PAD, PAD), :] = total
+    with jax.named_scope("band"):
+        for r in range(8):
+            p = pp[pl.ds(r * LANES, LANES), :]
+            total = None
+            for _ in range(3):
+                part = p.astype(BF16)
+                p = p - part.astype(F32)
+                d = lax.dot_general(
+                    band, part, (((1,), (1,)), ((), ())), preferred_element_type=F32
+                )
+                total = d if total is None else total + d
+            dd[pl.ds(r * PAD, PAD), :] = total
 
     @pl.loop(1, PEERS)
     def _(i):
         other, device = peer(i)
         remote(piece(dd, other), piece(c1, e), c1_s, c1_r, device).start()
 
-    means_over.wait_recv()
-    both = pl.ds(pl.multiple_of(e * 2 * PAD, PAD), 2 * PAD)
-
-    @pl.loop(1, PEERS)
-    def _(i):
-        remote(mm.at[both], mm.at[both], m2_s, m2_r, peer(i)[1]).start()
-
     piece(c1, e)[...] = piece(dd, e)[...]
-    wait_bytes(c1, (PEERS - 1) * PAD, c1_r)
+    with jax.named_scope("c1_wait"):
+        wait_bytes(c1, (PEERS - 1) * PAD, c1_r)
     total = c1[pl.ds(0, PAD), :]
     for i in range(1, PEERS):
         total = total + c1[pl.ds(i * PAD, PAD), :]
@@ -331,20 +346,16 @@
 
     piece(c2, me)[...] = total
 
-    wait_bytes(mm, (PEERS - 1) * 2 * PAD, m2_r)
-    turn = lax.rem(LANES - tile * 8, LANES)
-
-    def mine(rows):
-        return pltpu.roll(rows, turn, 1)[:, :8]
-
-    for b in range(BASINS):
-        for z in range(2):
-            rows = mm[pl.ds(z * PAD + b, 8, stride=2 * PAD), :]
-            psi_out[b, pl.ds(z * 8, 8), :] = mine(rows)
-    heat_out[pl.ds(0, 8), :] = mine(mm[pl.ds(BASINS, 8, stride=2 * PAD), :])
-    heat_out[pl.ds(8, 2), :] = mine(mm[pl.ds(PAD + BASINS, 8, stride=2 * PAD), :])[:2]
-
-    wait_bytes(c2, (SPREAD - 1) * PAD, c2_r)
+    with jax.named_scope("mean_wait"):
+        means_over.wait_recv()
+    both = pl.ds(pl.multiple_of(e * 2 * PAD, PAD), 2 * PAD)
+
+    @pl.loop(1, PEERS)
+    def _(i):
+        remote(mm.at[both], mm.at[both], m2_s, m2_r, peer(i)[1]).start()
+
+    with jax.named_scope("c2_wait"):
+        wait_bytes(c2, (SPREAD - 1) * PAD, c2_r)
     total = c2[pl.ds(0, PAD), :]
     for i in range(1, SPREAD):
         total = total + c2[pl.ds(i * PAD, PAD), :]
@@ -357,18 +368,32 @@
 
     piece(df, e)[...] = s2[...]
 
-    for m in range(MINE):
-        core_copy(m).wait_send()
-        for c in x_copies(m).values():
-            c().wait_send()
-        wait_bytes(ys, (SPREAD - 1) * PAD, yz_s.at[m])
-    means_over.wait_send()
-    wait_bytes(c1, (PEERS - 1) * PAD, c1_s)
-    wait_bytes(mm, (PEERS - 1) * 2 * PAD, m2_s)
-    wait_bytes(c2, (SPREAD - 1) * PAD, c2_s)
-    wait_bytes(df, (PEERS - 1) * PAD, c3_s)
-
-    wait_bytes(df, (PEERS - 1) * PAD, c3_r)
+    with jax.named_scope("mm_wait"):
+        wait_bytes(mm, (PEERS - 1) * 2 * PAD, m2_r)
+    turn = lax.rem(LANES - tile * 8, LANES)
+    with jax.named_scope("mean_out"):
+        for b in range(BASINS):
+            rows = [mm[pl.ds(z * PAD + b, 8, stride=2 * PAD), :] for z in range(2)]
+            rows = pltpu.roll(jnp.concatenate(rows, axis=0), turn, 1)
+            psi_out[b] = jnp.swapaxes(rows, 0, 1)[:8, :]
+        rows = [mm[pl.ds(z * PAD + BASINS, 8, stride=2 * PAD), :] for z in range(2)]
+        rows = pltpu.roll(jnp.concatenate(rows, axis=0), turn, 1)
+        heat_out[...] = jnp.swapaxes(rows, 0, 1)[:8, :BASINS]
+
+    with jax.named_scope("send_wait"):
+        for m in range(MINE):
+            core_copy(m).wait_send()
+            for c in x_copies(m).values():
+                c().wait_send()
+            wait_bytes(ys, (SPREAD - 1) * PAD, yz_s.at[m])
+        means_over.wait_send()
+        wait_bytes(c1, (PEERS - 1) * PAD, c1_s)
+        wait_bytes(mm, (PEERS - 1) * 2 * PAD, m2_s)
+        wait_bytes(c2, (SPREAD - 1) * PAD, c2_s)
+        wait_bytes(df, (PEERS - 1) * PAD, c3_s)
+
+    with jax.named_scope("c3_wait"):
+        wait_bytes(df, (PEERS - 1) * PAD, c3_r)
     for c in range(NBANDS):
         rows = df[pl.ds(c, 8, stride=PAD), :]
         for q in range(4):
@@ -383,26 +408,33 @@
     return a.reshape(-1, LANES)
 
 
+def finish(psi, heat, cov, psi_out, heat_out, cov_out, sem):
+    copies = [
+        pltpu.make_async_copy(a, b, sem.at[i])
+        for i, (a, b) in enumerate(((psi, psi_out), (heat, heat_out), (cov, cov_out)))
+    ]
+    for c in copies:
+        c.start()
+    for c in copies:
+        c.wait()
+
+
 def local(v, h, t, lab, zone):
-    lats = v.shape[-1]
-    columns = COLS * 16
-    spacing = (metric_factor(lats) / math.sqrt(columns)).reshape(8, LANES)
     vmem = lambda *s: pltpu.VMEM(s, F32)
     big = MINE * LAYERS * COLS * 8
     dma = pltpu.SemaphoreType.DMA
     anywhere = pl.BlockSpec(memory_space=pl.ANY)
     inside = pl.BlockSpec(memory_space=pltpu.VMEM)
-    psi, heat, cov = pl.pallas_call(
+    shapes = ((BASINS, 8, LAYERS), (8, BASINS), (NBANDS, MEMBERS, MEMBERS))
+    outs = pl.pallas_call(
         kernel,
-        out_shape=(
-            jax.ShapeDtypeStruct((BASINS, LAYERS, 8), F32),
-            jax.ShapeDtypeStruct((BASINS, 8), F32),
-            jax.ShapeDtypeStruct((NBANDS, MEMBERS, MEMBERS), F32),
-        ),
-        in_specs=[anywhere] * 3 + [inside] * 3,
+        out_shape=tuple(pltpu.VMEM(s, F32) for s in shapes),
+        in_specs=[anywhere] * 5,
         out_specs=(inside, inside, inside),
         scratch_shapes=[
             vmem(big, LANES), vmem(big, LANES), vmem(big, LANES),
+            pltpu.VMEM((COLS * 8, LANES), jnp.int32),
+            pltpu.VMEM((8, LANES), jnp.int32),
             vmem(COLS * BASINS, 8, LANES),
             vmem(COLS, 8, LANES),
             vmem(MINE, 2, LAYERS // 2, ROWS, 8, LANES),
@@ -425,16 +457,27 @@
             vmem(PEERS * PAD, LANES),
             vmem(PAD, LANES),
             vmem(PEERS * 2 * PAD, LANES),
-            dma((MINE, 3)),
+            dma((MINE, 3)), dma((2,)),
             dma((MINE,)), dma((MINE,)),
             dma((MINE, 6)), dma((MINE, 6)),
             dma((MINE,)), dma((MINE,)),
             dma, dma, dma, dma, dma, dma, dma, dma, dma, dma,
         ],
-        compiler_params=pltpu.CompilerParams(collective_id=0, has_side_effects=True),
+        compiler_params=pltpu.CompilerParams(
+            collective_id=0, has_side_effects=True, vmem_limit_bytes=60 << 20
+        ),
         name="overturning",
-    )(lat_tiles(v), lat_tiles(h), lat_tiles(t), lat_tiles(lab), zone.reshape(8, LANES), spacing)
-    return psi, heat, cov
+    )(lat_tiles(v), lat_tiles(h), lat_tiles(t), lat_tiles(lab), zone.reshape(8, LANES))
+    psi, heat, cov = pl.pallas_call(
+        finish,
+        out_shape=tuple(jax.ShapeDtypeStruct(s, F32) for s in shapes),
+        in_specs=[inside] * 3,
+        out_specs=(anywhere,) * 3,
+        scratch_shapes=[dma((3,))],
+        compiler_params=pltpu.CompilerParams(vmem_limit_bytes=1 << 20),
+        name="finish",
+    )(*outs)
+    return jnp.swapaxes(psi, 1, 2), jnp.swapaxes(heat, 0, 1), cov
 
 
 def solution(mesh):

time: 51.7 us -> 45.6 us (0.88)
  local copies, waits for them, and re-layouts: 4.62 us -> 0 us
  other arithmetic: 0.65 us -> 0 us
  Pallas kernels: 45.5 us -> 44.9 us
    pallas_call x2 -> x0, local copies, waits for them, and re-layouts: 2.95 us -> none  [local(): pl.pallas_call(kernel, out_shape=(jax.ShapeDtypeStruct((BASINS, LAYERS, 8...]
    unnamed x1 -> x0, local copies, waits for them, and re-layouts: 1.67 us -> none
    div x1 -> x0, other arithmetic: 0.65 us -> none  [local(): spacing = (metric_factor(lats) / math.sqrt(columns)).reshape(8, LANES)]
    pallas_call x1 -> x2, Pallas kernels: 45.5 us -> 44.9 us  [the longest x1 44.1 us: local(): pl.pallas_call(kernel, out_shape=tuple((pltpu.VMEM(s, F32) for s in shape...]
where the time goes in v2:
time: 45.6 us; the launch traced here: 45.5 us
  Pallas kernels  44.9 us (98%)
  between operations  0.64 us (1%)
    pallas_call x1, Pallas kernels, local(): pl.pallas_call(kernel, out_shape=tuple((pltpu.VMEM(s, F32) for s in shape...  44.1 us

profile of v2, /device:TPU:1, one launch (start us, length us, event | category | flops | bytes accessed | tf_op | source)
XLA Modules:
  0.0 45.5 jit_solution(14843505902587925189)
XLA Ops:
  0.6 44.1 %overturning.1 = (f32[10,8,16]{2,1,0:T(8,128)S(1)}, f32[8,10]{1,0:T(8,128)S(1)}, f32[16,32,32]{2,1,0:T(8,128)S(1)}) custom-call(f32[4096,128]{1,0:T(8,128)} %bitcast.23, f32[4096,128]{1,0:T(8,128)} %bitcast.24, f32[4096,128]{1,0:T(8,128)} %bitcast.25, s32[64,128]{1,0:T(8,128)} %bitcast.26, s32[8,128]{1,0:T(8,128)} %bitcast.27), custom_call_target="tpu_custom_call" | custom-call | tf_op jit(solution)/shard_map/overturning/pallas_call | solution.py:429
  44.8 0.7 %finish.1 = (f32[10,8,16]{2,1,0:T(8,128)}, f32[8,10]{1,0:T(8,128)}, f32[16,32,32]{2,1,0:T(8,128)}) custom-call(f32[10,8,16]{2,1,0:T(8,128)S(1)} %get-tuple-element.9.psi, f32[8,10]{1,0:T(8,128)S(1)} %get-tuple-element.10.heat, f32[16,32,32]{2,1,0:T(8,128)S(1)} %get-tuple-element.11.cov), custom_call_target="tpu_custom_call" | custom-call | tf_op jit(solution)/shard_map/finish/pallas_call | solution.py:471

commit v3 on v2

--- a/solution.py
+++ b/solution.py
@@ -24,6 +24,10 @@
 RING = 4
 PEERS = 8
 SPREAD = 16
+TURNED = (1,)
+WIDE = RING * BASINS
+FAR_PEERS = (4, 3, 5, 2, 6, 1, 7)
+FAR_SPREAD = (12, 4, 13, 11, 5, 3, 14, 10, 6, 2, 8, 15, 9, 7, 1)
 
 
 def metric_factor(row):
@@ -36,10 +40,10 @@
 def kernel(
     v_hbm, h_hbm, t_hbm, lab_hbm, zone_hbm,
     psi_out, heat_out, cov_out,
-    vb, hb, tb, lab_ref, zone_ref, onehot, heat_cols, ps, cr, xs, fa, fb, na, nb, rl, ys, rb,
-    an, pp, dd, c1, s1, c2, s2, df, mb, mm,
+    vb, hb, tb, lab_ref, zone_ref, onehot, heat_cols, ps, cr, xs, fa, fb, na, nb, rl,
+    ys, rb, yf, rf, an, dd, c1, s1, c2, s2, df, mb, mm,
     hbm_sem, small_sem, core_s, core_r, x_s, x_r, yz_s, yz_r,
-    c1_s, c1_r, c2_s, c2_r, c3_s, c3_r, m1_s, m1_r, m2_s, m2_r,
+    c_s, c1_r, c2_r, c3_r, m1_r, m2_r,
 ):
     member = lax.axis_index("member")
     tile = lax.axis_index("tile")
@@ -69,13 +73,17 @@
             device_id=device, device_id_type=MESH,
         )
 
+    def wait_bytes(ref, rows, sem):
+        view = ref.at[pl.ds(0, rows)]
+        pltpu.make_async_copy(view, view, sem).wait()
+
     chunk = LAYERS * COLS * 8
 
     def load(m):
         rows = pl.ds(m * chunk, chunk)
         return [
-            pltpu.make_async_copy(a.at[rows], b.at[rows], hbm_sem.at[m, i])
-            for i, (a, b) in enumerate(((v_hbm, vb), (h_hbm, hb), (t_hbm, tb)))
+            pltpu.make_async_copy(a.at[rows], b.at[rows], hbm_sem.at[m])
+            for a, b in ((v_hbm, vb), (h_hbm, hb), (t_hbm, tb))
         ]
 
     labels = pltpu.make_async_copy(lab_hbm, lab_ref, small_sem.at[0])
@@ -108,10 +116,12 @@
     def rows_of(m):
         return ROWS if m == MINE - 1 else BASINS
 
+    def half_of(m):
+        return BASINS // 2 if m in TURNED else rows_of(m)
+
     def compute(m):
         with jax.named_scope("hbm_wait"):
-            for c in load(m):
-                c.wait()
+            wait_bytes(vb, 3 * chunk, hbm_sem.at[m])
         if m + 2 < MINE:
             for c in load(m + 2):
                 c.start()
@@ -154,7 +164,7 @@
         n = rows_of(m)
         return remote(
             ps.at[m, 1 - core, :, pl.ds(0, n)], cr.at[m, :, pl.ds(0, n)],
-            core_s.at[m], core_r.at[m], sibling,
+            core_s, core_r.at[m], sibling,
         )
 
     right, left = along_x(1), along_x(-1)
@@ -163,20 +173,29 @@
     at_far = lax.rem(x + 2, RING)
 
     def x_copies(m):
-        n = pl.ds(0, rows_of(m))
+        n = pl.ds(0, half_of(m))
         hi = RING
 
         def c(i, src, dst, device):
-            return lambda: remote(src, dst, x_s.at[m, i], x_r.at[m, i], device)
+            return lambda: remote(src, dst, x_s, x_r.at[m, i], device)
 
         return dict(
             far_right=c(0, xs.at[m, at_far, n], fa.at[m, n], right),
             far_left=c(1, xs.at[m, hi + at_far, n], fb.at[m, n], left),
             near_right=c(2, xs.at[m, hi + at_right, n], na.at[m, 1, n], right),
-            near_left=c(3, xs.at[m, at_left, n], nb.at[m, 0, n], left),
-            sum_right=c(4, rl.at[m, 0, n], na.at[m, 0, n], right),
-            sum_left=c(5, rl.at[m, 1, n], nb.at[m, 1, n], left),
+            near_left=c(2, xs.at[m, at_left, n], nb.at[m, 0, n], left),
+            sum_right=c(2, rl.at[m, 0, n], na.at[m, 0, n], right),
+            sum_left=c(2, rl.at[m, 1, n], nb.at[m, 1, n], left),
         )
+
+    def start_x(m):
+        copies = x_copies(m)
+        for name in ("far_right", "far_left", "near_right", "near_left"):
+            copies[name]().start()
+
+    def near_wait(m):
+        with jax.named_scope("near_wait"):
+            wait_bytes(vb, 4 * half_of(m) * 8, x_r.at[m, 2])
 
     def pair_sum(m):
         with jax.named_scope("core_wait"):
@@ -188,15 +207,13 @@
                 xs[m, kk, r] = ps[m, core, kk, r] + cr[m, kk, r]
             return 0
 
-        copies = x_copies(m)
         with jax.named_scope("pair_sum"):
             lax.fori_loop(0, LAYERS // 2, one, 0)
-        for name in ("far_right", "far_left", "near_right", "near_left"):
-            copies[name]().start()
+        start_x(m)
 
     def relay(m):
         copies = x_copies(m)
-        n = rows_of(m)
+        n = half_of(m)
         with jax.named_scope("far_wait"):
             copies["far_right"]().wait_recv()
         for r in range(n):
@@ -208,38 +225,72 @@
             rl[m, 1, r] = xs[m, RING + at_left, r] + fb[m, r]
         copies["sum_left"]().start()
 
-    def piece(ref, i):
-        return ref.at[pl.ds(pl.multiple_of(i * PAD, PAD), PAD)]
+    def piece(ref, i, rows=PAD):
+        return ref.at[pl.ds(pl.multiple_of(i * rows, 8), rows)]
 
     def spread_out(m):
-        copies = x_copies(m)
         n = rows_of(m)
-        with jax.named_scope("near_wait"):
-            for name in ("near_right", "near_left", "sum_right", "sum_left"):
-                copies[name]().wait_recv()
+        near_wait(m)
         for z in range(2):
             for r in range(n):
                 total = xs[m, z * RING + x, r] + (na[m, z, r] + nb[m, z, r])
                 ys[pl.ds((m * SPREAD + z * GROUPS) * PAD + r, 8, stride=PAD), :] = total
-        for r in range(n, PAD):
-            for z in range(2):
-                ys[pl.ds((m * SPREAD + z * GROUPS) * PAD + r, 8, stride=PAD), :] = zero
-
-        @pl.loop(1, SPREAD)
-        def _(i):
+        for i in FAR_SPREAD:
             other, device = spread(i)
             remote(
                 piece(ys, m * SPREAD + other), piece(rb, me * MINE + m),
-                yz_s.at[m], yz_r.at[m], device,
+                yz_s, yz_r.at[m], device,
             ).start()
-
         piece(rb, me * MINE + m)[...] = piece(ys, m * SPREAD + me)[...]
 
-    def wait_bytes(ref, rows, sem):
-        view = ref.at[pl.ds(0, rows)]
-        pltpu.make_async_copy(view, view, sem).wait()
+    def turn_out(m):
+        with jax.named_scope("core_wait"):
+            core_copy(m).wait_recv()
+        base = TURNED.index(m) * SPREAD
+
+        def one(kk, _):
+            at = (base + lax.div(kk, RING) * GROUPS) * WIDE + lax.rem(kk, RING) * BASINS
+            for r in range(BASINS):
+                total = ps[m, core, kk, r] + cr[m, kk, r]
+                yf[pl.ds(at + r, 8, stride=WIDE), :] = total
+            return 0
+
+        with jax.named_scope("turn_sum"):
+            lax.fori_loop(0, LAYERS // 2, one, 0)
+        for i in FAR_SPREAD:
+            other, device = spread(i)
+            remote(
+                piece(yf, base + other, WIDE), piece(rf, base + me, WIDE),
+                yz_s, yz_r.at[m], device,
+            ).start()
+        piece(rf, base + me, WIDE)[...] = piece(yf, base + me, WIDE)[...]
+
+    def turn_in(m):
+        with jax.named_scope("turn_wait"):
+            wait_bytes(vb, (SPREAD - 1) * WIDE, yz_r.at[m])
+        base = TURNED.index(m) * SPREAD * WIDE
+        for k in range(RING):
+            for b in range(BASINS):
+                at = base + k * BASINS + b
+                half, r = divmod(b, BASINS // 2)
+                xs[m, half * RING + k, r] = (
+                    rf[pl.ds(at, 8, stride=WIDE), :]
+                    + rf[pl.ds(at + GROUPS * WIDE, 8, stride=WIDE), :]
+                )
+        start_x(m)
+
+    def turn_end(m):
+        near_wait(m)
+        for b in range(BASINS):
+            half, r = divmod(b, BASINS // 2)
+            total = xs[m, half * RING + x, r] + (na[m, half, r] + nb[m, half, r])
+            rb[pl.ds(m * PAD + b, 8, stride=MINE * PAD), :] = total
 
     spacing = metric_factor(member)
+
+    for m in TURNED:
+        for b in range(BASINS):
+            rb[pl.ds((MEMBERS + m) * PAD + b, 8, stride=MINE * PAD), :] = zero
 
     compute(0)
     with jax.named_scope("entry"):
@@ -250,24 +301,25 @@
     pair_sum(0)
     compute(2)
     core_copy(2).start()
-    pair_sum(1)
-    relay(0)
+    turn_out(1)
+    pair_sum(2)
     compute(3)
     core_copy(3).start()
-    pair_sum(2)
-    relay(1)
+    relay(0)
     pair_sum(3)
+    relay(2)
     spread_out(0)
-    relay(2)
-    spread_out(1)
+    turn_in(1)
     relay(3)
     spread_out(2)
+    relay(1)
     spread_out(3)
+    turn_end(1)
     with jax.named_scope("yz_wait"):
         for m in range(MINE):
-            wait_bytes(ys, (SPREAD - 1) * PAD, yz_r.at[m])
-
-    with jax.named_scope("anomaly"):
+            if m not in TURNED:
+                wait_bytes(vb, (SPREAD - 1) * PAD, yz_r.at[m])
+
         for b in range(BASINS):
             a = []
             for q in range(4):
@@ -289,48 +341,46 @@
 
     mm[pl.ds(pl.multiple_of((e * 2 + z_hi) * PAD, PAD), PAD), :] = mb[...]
     means_over = remote(
-        mb, piece(mm, e * 2 + z_hi), m1_s, m1_r,
+        mb, piece(mm, e * 2 + z_hi), c_s, m1_r,
         {"member": member, "tile": (1 - z_hi) * PEERS + e},
     )
     means_over.start()
-
-    def gram(n, _):
-        acc = [None] * 4
-        for b in range(BASINS):
-            row = jnp.broadcast_to(an[pl.ds(b * MEMBERS + n, 1), :], (8, LANES))
-            for q in range(4):
-                t = row * an[pl.ds(b * MEMBERS + q * 8, 8), :]
-                acc[q] = t if acc[q] is None else acc[q] + t
-        at = pl.multiple_of((n % 8) * LANES + (n // 8) * MEMBERS, MEMBERS)
-        for q in range(4):
-            pp[pl.ds(at + q * 8, 8), :] = acc[q]
-        return 0
-
-    with jax.named_scope("gram"):
-        lax.fori_loop(0, MEMBERS, gram, 0)
 
     zones.wait()
     zone = jnp.broadcast_to(zone_ref[pl.ds(member, 1), :], (NBANDS, LANES))
     band = jnp.where(
         zone == lax.broadcasted_iota(jnp.int32, (NBANDS, LANES), 0), 1.0, 0.0
     ).astype(BF16)
-    with jax.named_scope("band"):
-        for r in range(8):
-            p = pp[pl.ds(r * LANES, LANES), :]
-            total = None
-            for _ in range(3):
-                part = p.astype(BF16)
-                p = p - part.astype(F32)
-                d = lax.dot_general(
-                    band, part, (((1,), (1,)), ((), ())), preferred_element_type=F32
-                )
-                total = d if total is None else total + d
-            dd[pl.ds(r * PAD, PAD), :] = total
-
-    @pl.loop(1, PEERS)
-    def _(i):
+    band = jnp.concatenate([band] * 3, axis=1)
+
+    @pl.loop(0, PEERS)
+    def _(t):
+        step = lax.div(t + 1, 2)
+        i = PEERS // 2 + step * (1 - 2 * lax.rem(t, 2))
         other, device = peer(i)
-        remote(piece(dd, other), piece(c1, e), c1_s, c1_r, device).start()
+        acc = [[None] * 4 for _ in range(4)]
+        for b in range(BASINS):
+            a = [an[pl.ds(b * MEMBERS + q * 8, 8), :] for q in range(4)]
+            for k in range(4):
+                row = an[pl.ds(b * MEMBERS + k * 8 + other, 1), :]
+                row = jnp.broadcast_to(row, (8, LANES))
+                for q in range(4):
+                    p = row * a[q]
+                    acc[k][q] = p if acc[k][q] is None else acc[k][q] + p
+        p = jnp.concatenate([v for row in acc for v in row], axis=0)
+        parts = []
+        for _ in range(3):
+            parts.append(p.astype(BF16))
+            p = p - parts[-1].astype(F32)
+        d = lax.dot_general(
+            band, jnp.concatenate(parts, axis=1), (((1,), (1,)), ((), ())),
+            preferred_element_type=F32,
+        )
+        piece(dd, other)[...] = d
+
+        @pl.when(t < PEERS - 1)
+        def _():
+            remote(piece(dd, other), piece(c1, e), c_s, c1_r, device).start()
 
     piece(c1, e)[...] = piece(dd, e)[...]
     with jax.named_scope("c1_wait"):
@@ -340,9 +390,8 @@
         total = total + c1[pl.ds(i * PAD, PAD), :]
     s1[...] = total
 
-    @pl.loop(1, SPREAD)
-    def _(i):
-        remote(s1, piece(c2, me), c2_s, c2_r, spread(i)[1]).start()
+    for i in FAR_SPREAD:
+        remote(s1, piece(c2, me), c_s, c2_r, spread(i)[1]).start()
 
     piece(c2, me)[...] = total
 
@@ -350,9 +399,8 @@
         means_over.wait_recv()
     both = pl.ds(pl.multiple_of(e * 2 * PAD, PAD), 2 * PAD)
 
-    @pl.loop(1, PEERS)
-    def _(i):
-        remote(mm.at[both], mm.at[both], m2_s, m2_r, peer(i)[1]).start()
+    for i in FAR_PEERS:
+        remote(mm.at[both], mm.at[both], c_s, m2_r, peer(i)[1]).start()
 
     with jax.named_scope("c2_wait"):
         wait_bytes(c2, (SPREAD - 1) * PAD, c2_r)
@@ -362,9 +410,8 @@
     norm = float((MEMBERS - 1) * BASINS * LAYERS * (8 * LANES // NBANDS))
     s2[...] = total * (1.0 / norm)
 
-    @pl.loop(1, PEERS)
-    def _(i):
-        remote(s2, piece(df, e), c3_s, c3_r, peer(i)[1]).start()
+    for i in FAR_PEERS:
+        remote(s2, piece(df, e), c_s, c3_r, peer(i)[1]).start()
 
     piece(df, e)[...] = s2[...]
 
@@ -381,16 +428,11 @@
         heat_out[...] = jnp.swapaxes(rows, 0, 1)[:8, :BASINS]
 
     with jax.named_scope("send_wait"):
-        for m in range(MINE):
-            core_copy(m).wait_send()
-            for c in x_copies(m).values():
-                c().wait_send()
-            wait_bytes(ys, (SPREAD - 1) * PAD, yz_s.at[m])
-        means_over.wait_send()
-        wait_bytes(c1, (PEERS - 1) * PAD, c1_s)
-        wait_bytes(mm, (PEERS - 1) * 2 * PAD, m2_s)
-        wait_bytes(c2, (SPREAD - 1) * PAD, c2_s)
-        wait_bytes(df, (PEERS - 1) * PAD, c3_s)
+        straight = [m for m in range(MINE) if m not in TURNED]
+        wait_bytes(vb, 8 * sum(rows_of(m) for m in range(MINE)) * LAYERS // 2, core_s)
+        wait_bytes(vb, 8 * 6 * sum(half_of(m) for m in range(MINE)), x_s)
+        wait_bytes(vb, (SPREAD - 1) * (len(straight) * PAD + len(TURNED) * WIDE), yz_s)
+        wait_bytes(vb, ((PEERS - 1) * 4 + SPREAD) * PAD, c_s)
 
     with jax.named_scope("c3_wait"):
         wait_bytes(df, (PEERS - 1) * PAD, c3_r)
@@ -447,8 +489,9 @@
             vmem(MINE, 2, ROWS, 8, LANES),
             vmem(MINE * SPREAD * PAD, LANES),
             vmem(MINE * SPREAD * PAD, LANES),
+            vmem(len(TURNED) * SPREAD * WIDE, LANES),
+            vmem(len(TURNED) * SPREAD * WIDE, LANES),
             vmem(BASINS * MEMBERS, LANES),
-            vmem(MEMBERS * MEMBERS, LANES),
             vmem(PEERS * PAD, LANES),
             vmem(PEERS * PAD, LANES),
             vmem(PAD, LANES),
@@ -457,11 +500,11 @@
             vmem(PEERS * PAD, LANES),
             vmem(PAD, LANES),
             vmem(PEERS * 2 * PAD, LANES),
-            dma((MINE, 3)), dma((2,)),
-            dma((MINE,)), dma((MINE,)),
-            dma((MINE, 6)), dma((MINE, 6)),
-            dma((MINE,)), dma((MINE,)),
-            dma, dma, dma, dma, dma, dma, dma, dma, dma, dma,
+            dma((MINE,)), dma((2,)),
+            dma, dma((MINE,)),
+            dma, dma((MINE, 3)),
+            dma, dma((MINE,)),
+            dma, dma, dma, dma, dma, dma,
         ],
         compiler_params=pltpu.CompilerParams(
             collective_id=0, has_side_effects=True, vmem_limit_bytes=60 << 20

time: 45.6 us -> 41.9 us (0.919)
  Pallas kernels: 44.9 us -> 41.1 us
    pallas_call x1, Pallas kernels: 44.1 us -> 40.4 us  [local(): pl.pallas_call(kernel, out_shape=tuple((pltpu.VMEM(s, F32) for s in shape...]
where the time goes in v3:
time: 41.9 us; the launch traced here: 41.8 us
  Pallas kernels  41.1 us (98%)
  between operations  0.64 us (2%)
    pallas_call x1, Pallas kernels, local(): pl.pallas_call(kernel, out_shape=tuple((pltpu.VMEM(s, F32) for s in shape...  40.4 us

profile of v3, /device:TPU:1, one launch (start us, length us, event | category | flops | bytes accessed | tf_op | source)
XLA Modules:
  0.0 41.8 jit_solution(7601605598555137059)
XLA Ops:
  0.6 40.4 %overturning.1 = (f32[10,8,16]{2,1,0:T(8,128)S(1)}, f32[8,10]{1,0:T(8,128)S(1)}, f32[16,32,32]{2,1,0:T(8,128)S(1)}) custom-call(f32[4096,128]{1,0:T(8,128)} %bitcast.23, f32[4096,128]{1,0:T(8,128)} %bitcast.24, f32[4096,128]{1,0:T(8,128)} %bitcast.25, s32[64,128]{1,0:T(8,128)} %bitcast.26, s32[8,128]{1,0:T(8,128)} %bitcast.27), custom_call_target="tpu_custom_call" | custom-call | tf_op jit(solution)/shard_map/overturning/pallas_call | solution.py:471
  41.0 0.7 %finish.1 = (f32[10,8,16]{2,1,0:T(8,128)}, f32[8,10]{1,0:T(8,128)}, f32[16,32,32]{2,1,0:T(8,128)}) custom-call(f32[10,8,16]{2,1,0:T(8,128)S(1)} %get-tuple-element.9.psi, f32[8,10]{1,0:T(8,128)S(1)} %get-tuple-element.10.heat, f32[16,32,32]{2,1,0:T(8,128)S(1)} %get-tuple-element.11.cov), custom_call_target="tpu_custom_call" | custom-call | tf_op jit(solution)/shard_map/finish/pallas_call | solution.py:514
